TPU v7x, 256 devices: a whole 4x4x8 slice. The times are simulated.
256 devices in a mesh: row: 16 (over x_lo, z), col: 16 (over x_hi, y, core).
Axes of the slice: x: 4 (x_hi: 2, x_lo: 2; x = x_hi * 2 + x_lo), y: 4, z: 8, core: 2. Of those that a mesh axis runs over, the one named last changes fastest.
Arguments:
- forward_map: float32 [2048, 16384], P('row', 'col'), may hold values from -0.125 to 0.125
- sensor_weights: float32 [2048], P('row'), may hold values from 0.25 to 4
- sensor_mask: int32 [2048], P('row'), may hold values 0 or 1
Outputs:
- gram_matrix: float32 [16384, 16384], P('row', 'col')
All inputs are finite; a program needn't handle non-finite values. No bound on the sum of `sensor_mask` on one device may be relied on, other than what follows from the above.
Results may differ from a plain program's by a relative error of at most 0.000061.
Values sent between devices are 32-bit elements; how exact they have to be, the bound alone decides.
A program may use at most 128 MiB of HBM per device.

v0:
```python
import jax
import jax.numpy as jnp
from jax import lax
from jax.sharding import PartitionSpec as P


def contract(left_rows, right_rows):
    return lax.dot_general(
        left_rows,
        right_rows,
        (((0,), (0,)), ((), ())),
        precision=lax.Precision.HIGHEST,
        preferred_element_type=jnp.float32,
    )


def per_device(forward_map, sensor_weights, sensor_mask):
    sensor_scale = sensor_weights * sensor_mask.astype(jnp.float32)
    weighted = forward_map * sensor_scale[:, None]
    gathered = lax.all_gather(weighted, "row", axis=0, tiled=True)
    spread = lax.all_to_all(forward_map, "col", split_axis=0, concat_axis=1, tiled=True)
    regrouped = lax.all_to_all(spread, "row", split_axis=1, concat_axis=0, tiled=True)
    rows_count = lax.axis_size("row")
    cols_count = lax.axis_size("col")
    columns = gathered.shape[1]
    stride_rows = gathered.shape[0] // (rows_count * cols_count)
    permuted = (
        gathered.reshape(rows_count, cols_count, stride_rows, columns)
        .transpose(1, 0, 2, 3)
        .reshape(-1, columns)
    )
    return contract(lax.all_gather(regrouped, "col", axis=0, tiled=True), permuted)


def solution(mesh):
    placed = (P("row", "col"), P("row"), P("row"))
    return jax.shard_map(
        per_device, mesh=mesh, in_specs=placed, out_specs=P("row", "col"), check_vma=False
    )
```

profile of v0, /device:TPU:10, one launch (start us, length us, event | category | flops | bytes accessed | tf_op | source)
XLA Modules:
  0.0 249.8 jit_solution(12365117713609892817)
XLA Ops:
  6.5 0.0 all-gather.3.cloned.1.call-start
  6.5 0.7 convert_multiply_fusion
  7.2 1.9 broadcast_multiply_fusion
  9.1 0.0 all-gather.3.cloned.1.call-update
  9.2 0.0 all-gather.5.cloned.1.call-start
  9.2 15.2 %all_to_all.32 = f32[16,8,1024]{2,1,0:T(8,128)S(1)} all-to-all(f32[16,8,1024]{2,1,0:T(8,128)} %bitcast.15), channel_id=1, replica_groups=mesh['row'=16,'col'=16] {'col'}, dimensions={0} | all-to-all | bytes 1048576 | tf_op jit(solution)/shard_map/all_to_all | solution.py:21
  24.4 103.3 %all_to_all.33 = f32[8,16,1024]{2,0,1:T(8,128)} all-to-all(f32[8,16,1024]{2,0,1:T(8,128)S(1)} %bitcast.17), channel_id=1, replica_groups=mesh['row'=16,'col'=16] {'row'}, dimensions={1} | all-to-all | bytes 1048576 | tf_op jit(solution)/shard_map/all_to_all | solution.py:22
  127.7 0.0 all-gather.5.cloned.1.call-update
  127.7 0.0 all-gather.3.cloned.1.call-done
  127.7 8.3 %copy.6 = f32[16,16,8,1024]{3,2,1,0:T(8,128)} copy(f32[16,16,8,1024]{3,2,0,1:T(8,128)} %bitcast.13) | data formatting | bytes 16777216 | tf_op jit(solution)/shard_map/transpose | solution.py:29
  136.0 70.0 %all-gather.5.cloned.1.call-done = f32[2048,1024]{1,0:T(8,128)} async-done(((f32[128,1024]{1,0:T(8,128)}), f32[2048,1024]{1,0:T(8,128)}) %all-gather.5.cloned.1.call-update) | async-done | bytes 8388624 | tf_op jit(solution)/shard_map/all_gather | solution.py:32
  206.0 31.6 %convolution_bitcast_fusion = f32[1024,1024]{0,1:T(8,128)} fusion(f32[2048,1024]{1,0:T(8,128)} %bitcast.14, f32[2048,1024]{1,0:T(8,128)} %all-gather.5.cloned.1.call-done), kind=kOutput, calls=%fused_computation | convolution fusion | flops 25769803776 | bytes 20971520 | tf_op jit(solution)/shard_map/dot_general | solution.py:8
  237.6 5.3 %copy.7 = f32[1024,1024]{1,0:T(8,128)} copy(f32[1024,1024]{0,1:T(8,128)} %convolution_bitcast_fusion) | data formatting | bytes 8388608 | tf_op jit(solution)/shard_map/dot_general | solution.py:8
Async XLA Ops:
  6.5 121.2 %all-gather.3.cloned.1.call-start = ((), (), s32[]{:S(2)}) async-start(), calls=%async_computation.2 | async-start | bytes 8912896 | tf_op jit(solution)/shard_map/all_gather | solution.py:20
  9.2 196.8 %all-gather.5.cloned.1.call-start = ((), (), s32[]{:S(2)}) async-start(), calls=%async_computation.3 | async-start | bytes 8912896 | tf_op jit(solution)/shard_map/all_gather | solution.py:32
Sparse Core Ops, SparseCore 0:
  9.3 102.8 all-gather.2
  127.8 78.1 all-gather.4
where the time goes:
time: 254 us; the launch traced here: 250 us
  blocking collectives  118 us (46%)
  waiting for transfers between devices  70 us (28%)
  matrix products  31.6 us (12%)
  local copies, waits for them, and re-layouts  13.6 us (5%)
  between operations  13.4 us (5%)
  other arithmetic  2.61 us (1%)
    all_to_all x1, blocking collectives, per_device(): lax.all_to_all(spread, 'row', split_axis=1, concat_axis=0, tiled=True)  103 us
    all_gather x1, waiting for transfers between devices, per_device(): lax.all_gather(regrouped, 'col', axis=0, tiled=True)  70 us
    dot_general x1, matrix products, contract(): lax.dot_general(left_rows, right_rows, (((0,), (0,)), ((), ())), precisio...  31.6 us
    all_to_all x1, blocking collectives, per_device(): lax.all_to_all(forward_map, 'col', split_axis=0, concat_axis=1, tiled=True)  15.2 us
    transpose x1, local copies, waits for them, and re-layouts, per_device(): permuted = gathered.reshape(rows_count, cols_count, stride_rows, columns)...  8.26 us
    dot_general x1, local copies, waits for them, and re-layouts, contract(): lax.dot_general(left_rows, right_rows, (((0,), (0,)), ((), ())), precisio...  5.34 us
  transfers between devices with their start and end apart: 2, of which 1 were waited for; matrix products, arithmetic and copies ran while one was open for 3% of the time, Pallas kernels for 0%

commit v1 on v0

v1 whole, which is shorter than its diff:
```python
import functools

import jax
import jax.numpy as jnp
from jax import lax
from jax.experimental import pallas as pl
from jax.experimental.pallas import tpu as pltpu
from jax.sharding import PartitionSpec as P

MESH = pl.DeviceIdType.MESH
OBS, SIDE = 2048, 1024
PIECE, STEPS, CUTS = 16, 5, 8
SLOTS = STEPS * CUTS
TRIO = 3 * PIECE
LEFT = OBS

PARENT = ((0, 0, 0), (1, 2, 1), (4, 5, 5), (7, 3, 7), (6, 9, 10))

OUTER = (
    tuple((i, i) for i in range(0, 4)),
    tuple((i, i) for i in range(4, 10)),
    tuple((i, i) for i in range(10, 16)),
)
INNER = (
    ((0, 3), (3, 0), (1, 6), (6, 1)),
    ((5, 9), (9, 5), (7, 12), (12, 7), (2, 11), (11, 2)),
    ((4, 13), (13, 4), (8, 14), (14, 8), (10, 15), (15, 10)),
)
HOP = 3
LAG = 4 * HOP + 2
TURNS = SLOTS + LAG


def base_of(block):
    return 128 + CUTS * TRIO * ((block - 1) // 3) + PIECE * ((block - 1) % 3)


def row_of(block, cut):
    return PIECE * cut if block == 0 else base_of(block) + TRIO * cut


def pick(choice, values):
    out = values[-1]
    for i in reversed(range(len(values) - 1)):
        out = jnp.where(choice == i, values[i], out)
    return out


def kernel(
    map_ref, weights_ref, mask_ref, gram_ref,
    store, relay, scales, columns, right_hi, right_lo, left_hi, left_lo, total,
    load_sem, slot_sem, left_sem, left_own_sem, relay_sem, relay_own_sem, scale_sem,
    sent_sem, sent_scale_sem, plus_sem, minus_sem, twin_sem, cross_sem, toward_sem, onward_sem, out_sem,
):
    row, col = lax.axis_index("row"), lax.axis_index("col")
    x_lo, z = row // 8, row % 8
    x_hi, y, core = col // 8, (col // 2) % 4, col % 2
    up = (x_lo * 8 + (z + 1) % 8, col)
    down = (x_lo * 8 + (z + 7) % 8, col)
    pair = ((1 - x_lo) * 8 + z, col)
    plus = (row, x_hi * 8 + ((y + 1) % 4) * 2 + core)
    minus = (row, x_hi * 8 + ((y + 3) % 4) * 2 + core)
    twin = (row, x_hi * 8 + y * 2 + (1 - core))
    across = ((1 - x_lo) * 8 + z, (1 - x_hi) * 8 + y * 2 + core)
    links = (up, down, pair)
    outer = x_hi == x_lo
    inner = x_hi != x_lo
    first = core == z % 2
    dy = (y + 4 - z // 2) % 4

    def loading(cut):
        rows = pl.ds(PIECE * cut, PIECE)
        return pltpu.make_async_copy(map_ref.at[rows], store.at[rows], load_sem.at[cut])

    for cut in range(CUTS):
        loading(cut).start()
    scale = weights_ref[...] * mask_ref[...].astype(jnp.float32)
    scales[pl.ds(0, 8), :] = jnp.broadcast_to(scale, (8, 128))
    total[...] = jnp.zeros_like(total)

    barrier = pltpu.get_barrier_semaphore()
    for other in (up, down, pair, plus, minus, twin, across):
        pl.semaphore_signal(barrier, inc=1, device_id=other, device_id_type=MESH)
    pl.semaphore_wait(barrier, 7)

    def remote(source, target, sent, arrived, device):
        return pltpu.make_async_remote_copy(
            src_ref=source, dst_ref=target, send_sem=sent, recv_sem=arrived,
            device_id=device, device_id_type=MESH,
        )

    def arrival(ref, sem):
        return remote(ref, ref, sent_sem.at[0], sem, up)

    def span(start, size):
        return store.at[pl.ds(pl.multiple_of(start, 8), size)]

    def send_scale(source_block, step, g):
        remote(
            scales.at[pl.ds(8 * source_block, 8)],
            scales.at[pl.ds(pl.multiple_of(8 * (3 * step + 1 + g), 8), 8)],
            sent_scale_sem.at[0], scale_sem.at[step], links[g],
        ).start()

    for g in range(3):
        send_scale(0, 0, g)
    for cut in range(CUTS):
        loading(cut).wait()
        for g in range(3):
            remote(
                span(PIECE * cut, PIECE), span(128 + TRIO * cut + PIECE * g, PIECE),
                sent_sem.at[0], slot_sem.at[cut], links[g],
            ).start()

    def expand(block, start):
        square = jnp.broadcast_to(scales[pl.ds(pl.multiple_of(start, 8), 1), :], (128, 128))
        columns[block] = square.T

    back = (4 - dy) % 4
    hops = []
    for lane in range(4):
        on_outer = dy if lane % 2 == 0 else back
        on_inner = (1 + dy, 1 + back, pick(dy, (3, 2, 3, 4)), pick(dy, (3, 4, 3, 2)))[lane]
        hops.append(jnp.where(outer, on_outer, on_inner))
    goes_plus = (
        jnp.where(outer, dy <= 2, dy <= 2),
        inner & (dy < 0),
        jnp.where(outer, dy <= 2, (dy == 1) | (dy == 2)),
        inner & (dy == 3),
    )
    goes_minus = (
        inner & (dy < 0),
        jnp.where(outer, dy != 1, dy != 1),
        inner & (dy == 1),
        jnp.where(outer, dy != 1, (dy == 2) | (dy == 3)),
    )
    at_source = outer & (dy == 0) & first
    from_row = jnp.where(at_source, 0, LEFT)

    def pass_on(slot, source_row, device, sent):
        remote(
            span(source_row + 128 + TRIO * slot, TRIO), span(LEFT + 128 + TRIO * slot, TRIO),
            sent, left_sem.at[slot], device,
        ).start()

        @pl.when(slot < CUTS)
        def _():
            remote(
                span(source_row + PIECE * slot, PIECE), span(LEFT + PIECE * slot, PIECE),
                sent, left_own_sem.at[slot], device,
            ).start()

    def into_relay(slot, device, sent):
        fourth = slot // 4
        remote(
            span(128 + TRIO * slot, TRIO), relay.at[pl.ds(pl.multiple_of(TRIO * fourth, 8), TRIO)],
            sent, relay_sem.at[fourth], device,
        ).start()

        @pl.when(slot < CUTS)
        def _():
            remote(
                span(PIECE * slot, PIECE), relay.at[pl.ds(pl.multiple_of(480 + PIECE * fourth, 8), PIECE)],
                sent, relay_own_sem.at[fourth], device,
            ).start()

    def out_of_relay(slot):
        fourth = slot // 4
        held = relay.at[pl.ds(pl.multiple_of(TRIO * fourth, 8), TRIO)]
        arrival(held, relay_sem.at[fourth]).wait_recv()
        remote(held, span(LEFT + 128 + TRIO * slot, TRIO), onward_sem.at[0], left_sem.at[slot], across).start()

        @pl.when(slot < CUTS)
        def _():
            own = relay.at[pl.ds(pl.multiple_of(480 + PIECE * fourth, 8), PIECE)]
            arrival(own, relay_own_sem.at[fourth]).wait_recv()
            remote(own, span(LEFT + PIECE * slot, PIECE), onward_sem.at[0], left_own_sem.at[slot], across).start()

    def split(turn, start, phase, base, pieces):
        cut = turn - start

        @pl.when((turn >= start) & (turn < start + CUTS))
        def _():
            for n in range(pieces):
                (right_o, left_o), (right_i, left_i) = OUTER[phase][n], INNER[phase][n]

                def start_of(a, b):
                    def one(block):
                        return PIECE * cut if block == 0 else base_of(block) + TRIO * cut

                    return one(a) if a == b else jnp.where(outer, one(a), one(b))

                right_row = pl.multiple_of(start_of(right_o, right_i), 8)
                left_row = pl.multiple_of(LEFT + start_of(left_o, left_i), 8)
                block = right_o if right_o == right_i else jnp.where(outer, right_o, right_i)
                put = pl.ds(pl.multiple_of(base + PIECE * (pieces * cut + n), 16), PIECE)
                factor = columns[block, pl.ds(pl.multiple_of(PIECE * cut, 8), PIECE), :]
                for lane in range(SIDE // 128):
                    at = pl.ds(128 * lane, 128)
                    value = store[pl.ds(right_row, PIECE), at] * factor
                    high = value.astype(jnp.bfloat16)
                    right_hi[put, at] = high
                    right_lo[put, at] = (value - high.astype(jnp.float32)).astype(jnp.bfloat16)
                left_from = jnp.where(at_source, left_row - LEFT, left_row)
                value = store[pl.ds(pl.multiple_of(left_from, 8), PIECE), :]
                high = value.astype(jnp.bfloat16)
                left_hi[put, :] = high
                left_lo[put, :] = (value - high.astype(jnp.float32)).astype(jnp.bfloat16)

    def written(n):
        return pltpu.make_async_copy(total.at[n], gram_ref.at[:, pl.ds(256 * n, 256)], out_sem.at[n])

    def multiply(unit):
        k = pl.ds(pl.multiple_of(256 * unit, 256), 256)

        @pl.loop(0, 4)
        def _(n):
            at = pl.ds(pl.multiple_of(256 * n, 256), 256)

            def product(a, b):
                return lax.dot_general(
                    a[k, :], b[k, at], (((0,), (0,)), ((), ())), preferred_element_type=jnp.float32
                )

            total[n] += product(left_hi, right_hi) + product(left_hi, right_lo) + product(left_lo, right_hi)

            @pl.when(unit == 7)
            def _():
                written(n).start()

    @pl.loop(0, TURNS)
    def _(turn):
        step, cut, lane_now = turn // CUTS, turn % CUTS, turn % 4

        @pl.when(turn < SLOTS)
        def _():
            arrival(span(128 + TRIO * turn, TRIO), slot_sem.at[turn]).wait_recv()

            @pl.when(cut == 0)
            def _():
                arrival(scales.at[pl.ds(pl.multiple_of(8 + 24 * step, 8), 24)], scale_sem.at[step]).wait_recv()
                for g in range(3):
                    @pl.when(step < STEPS - 1)
                    def _():
                        source = pick(step, tuple(PARENT[s][g] for s in range(1, STEPS)))
                        remote(
                            scales.at[pl.ds(pl.multiple_of(8 * source, 8), 8)],
                            scales.at[pl.ds(pl.multiple_of(8 * (3 * step + 4 + g), 8), 8)],
                            sent_scale_sem.at[0], scale_sem.at[step + 1], links[g],
                        ).start()

            @pl.when(step < STEPS - 1)
            def _():
                for g in range(3):
                    base = pick(step, tuple(base_of(PARENT[s][g]) for s in range(1, STEPS)))
                    remote(
                        span(base + TRIO * cut, PIECE), span(128 + TRIO * (turn + CUTS) + PIECE * g, PIECE),
                        sent_sem.at[step + 1], slot_sem.at[turn + CUTS], links[g],
                    ).start()

            @pl.when(inner & first & (dy == 0))
            def _():
                @pl.when(lane_now < 2)
                def _():
                    pass_on(turn, 0, across, cross_sem.at[0])

                @pl.when(lane_now == 2)
                def _():
                    into_relay(turn, plus, toward_sem.at[0])

                @pl.when(lane_now == 3)
                def _():
                    into_relay(turn, minus, toward_sem.at[1])

        for lane, place in ((2, 1), (3, 3)):
            slot = turn - HOP

            @pl.when(inner & first & (dy == place) & (slot >= 0) & (slot < SLOTS) & ((slot + 4) % 4 == lane))
            def _():
                out_of_relay(slot)

        for lane in range(4):
            slot = turn - HOP * hops[lane] - jnp.where(first, 0, 1)

            @pl.when((slot >= 0) & (slot < SLOTS) & ((slot + 32) % 4 == lane))
            def _():
                @pl.when(jnp.logical_not(at_source))
                def _():
                    arrival(span(LEFT + 128 + TRIO * slot, TRIO), left_sem.at[slot]).wait_recv()

                    @pl.when(slot < CUTS)
                    def _():
                        arrival(span(LEFT + PIECE * slot, PIECE), left_own_sem.at[slot]).wait_recv()

                @pl.when(first & goes_plus[lane])
                def _():
                    pass_on(slot, from_row, plus, plus_sem.at[lane])

                @pl.when(first & goes_minus[lane])
                def _():
                    pass_on(slot, from_row, minus, minus_sem.at[lane])

                @pl.when(first)
                def _():
                    pass_on(slot, from_row, twin, twin_sem.at[lane])

        start_a, start_b, start_c = CUTS + LAG, 3 * CUTS + LAG, 4 * CUTS + LAG

        @pl.when(turn == start_a)
        def _():
            for block in range(10):
                expand(block, 8 * block)

        @pl.when(turn == start_c)
        def _():
            for block in range(10, 16):
                expand(block, 8 * block)

        @pl.when(turn == start_b)
        def _():
            for block in range(10, 13):
                expand(block, 8 * block)

        split(turn, start_a, 0, 0, 4)
        split(turn, start_b, 1, 512, 6)
        split(turn, start_c, 2, 1280, 6)
        in_a, in_b, in_c = turn - start_a, turn - start_b, turn - start_c
        due, unit = False, 0
        for at, number in (
            (start_a + 3, 0), (start_a + 7, 1),
            (start_b + 2, 2), (start_b + 5, 3), (start_b + 7, 4),
            (start_c + 2, 5), (start_c + 5, 6), (start_c + 7, 7),
        ):
            due = due | (turn == at)
            unit = jnp.where(turn == at, number, unit)

        @pl.when(due)
        def _():
            multiply(unit)

    for step in range(STEPS):
        remote(
            span(0, CUTS * TRIO), span(0, CUTS * TRIO), sent_sem.at[step], slot_sem.at[0], up
        ).wait_send()
    remote(
        scales.at[pl.ds(8, 120)], scales.at[pl.ds(8, 120)], sent_scale_sem.at[0], slot_sem.at[0], up
    ).wait_send()

    def drain(sem, rows):
        remote(span(0, rows), span(0, rows), sem, slot_sem.at[0], up).wait_send()

    for lane in range(4):
        @pl.when(first & goes_plus[lane])
        def _():
            drain(plus_sem.at[lane], 512)

        @pl.when(first & goes_minus[lane])
        def _():
            drain(minus_sem.at[lane], 512)

        @pl.when(first)
        def _():
            drain(twin_sem.at[lane], 512)

    @pl.when(inner & first & (dy == 0))
    def _():
        drain(cross_sem.at[0], 1024)
        drain(toward_sem.at[0], 512)
        drain(toward_sem.at[1], 512)

    @pl.when(inner & first & ((dy == 1) | (dy == 3)))
    def _():
        drain(onward_sem.at[0], 512)

    for n in range(4):
        written(n).wait()


def per_device(forward_map, sensor_weights, sensor_mask):
    dma = pltpu.SemaphoreType.DMA
    half = pltpu.VMEM((OBS, SIDE), jnp.bfloat16)
    return pl.pallas_call(
        kernel,
        out_shape=jax.ShapeDtypeStruct((SIDE, SIDE), jnp.float32),
        in_specs=[
            pl.BlockSpec(memory_space=pl.ANY),
            pl.BlockSpec(memory_space=pltpu.VMEM),
            pl.BlockSpec(memory_space=pltpu.VMEM),
        ],
        out_specs=pl.BlockSpec(memory_space=pl.ANY),
        scratch_shapes=[
            pltpu.VMEM((2 * OBS, SIDE), jnp.float32),
            pltpu.VMEM((512, SIDE), jnp.float32),
            pltpu.VMEM((128, 128), jnp.float32),
            pltpu.VMEM((16, 128, 128), jnp.float32),
            half, half, half, half,
            pltpu.VMEM((4, SIDE, 256), jnp.float32),
            dma((CUTS,)), dma((SLOTS,)), dma((SLOTS,)), dma((CUTS,)), dma((10,)), dma((2,)), dma((STEPS,)),
            dma((STEPS,)), dma((1,)), dma((4,)), dma((4,)), dma((4,)), dma((1,)), dma((2,)), dma((1,)), dma((4,)),
        ],
        compiler_params=pltpu.CompilerParams(
            collective_id=0, has_side_effects=True, vmem_limit_bytes=56 * 1024 * 1024
        ),
        cost_estimate=pl.CostEstimate(
            flops=2 * OBS * SIDE * SIDE, bytes_accessed=8 * SIDE * SIDE, transcendentals=0
        ),
    )(forward_map, sensor_weights.reshape(1, -1), sensor_mask.reshape(1, -1))


def solution(mesh):
    placed = (P("row", "col"), P("row"), P("row"))
    return jax.shard_map(
        per_device, mesh=mesh, in_specs=placed, out_specs=P("row", "col"), check_vma=False
    )
```

time: 254 us -> 108 us (0.43); the launches traced: 250 us -> 108 us
  blocking collectives: 118 us -> 0 us
  Pallas kernels: 0 us -> 103 us
  waiting for transfers between devices: 70 us -> 0 us
  matrix products: 31.6 us -> 0 us
  between operations: 13.4 us -> 0.01 us
  local copies, waits for them, and re-layouts: 13.6 us -> 4.79 us
  other arithmetic: 2.61 us -> 0 us
    all_to_all x2 -> x0, blocking collectives: 118 us -> none  [the longest x1 103 us: per_device(): lax.all_to_all(spread, 'row', split_axis=1, concat_axis=0, tiled=True)]
    pallas_call x0 -> x1, Pallas kernels: none -> 103 us  [per_device(): pl.pallas_call(kernel, out_shape=jax.ShapeDtypeStruct((SIDE, SIDE), jnp.f...]
    all_gather x2 -> x0, waiting for transfers between devices: 70 us -> none  [the longest x1 70 us: per_device(): lax.all_gather(regrouped, 'col', axis=0, tiled=True)]
    dot_general x1 -> x0, matrix products: 31.6 us -> none  [contract(): lax.dot_general(left_rows, right_rows, (((0,), (0,)), ((), ())), precisio...]
    transpose x1 -> x0, local copies, waits for them, and re-layouts: 8.26 us -> none  [per_device(): permuted = gathered.reshape(rows_count, cols_count, stride_rows, columns)...]
    dot_general x1 -> x0, local copies, waits for them, and re-layouts: 5.34 us -> none  [contract(): lax.dot_general(left_rows, right_rows, (((0,), (0,)), ((), ())), precisio...]
    unnamed x0 -> x1, local copies, waits for them, and re-layouts: none -> 4.79 us
    mul x2 -> x0, other arithmetic: 2.61 us -> none  [the longest x1 1.94 us: per_device(): weighted = forward_map * sensor_scale[:, None]]
  transfers between devices with their start and end apart: 2 -> 0, of which waited for: 1 -> 0; matrix products, arithmetic and copies ran while one was open for 3% -> 0% of each run, Pallas kernels for 0% -> 0%
where the time goes in v1:
time: 108 us
  Pallas kernels  103 us (95%)
  local copies, waits for them, and re-layouts  4.79 us (4%)
    pallas_call x1, Pallas kernels, per_device(): pl.pallas_call(kernel, out_shape=jax.ShapeDtypeStruct((SIDE, SIDE), jnp.f...  103 us
    unnamed x1, local copies, waits for them, and re-layouts  4.79 us

profile of v1, /device:TPU:10, one launch (start us, length us, event | category | flops | bytes accessed | tf_op | source)
XLA Modules:
  0.0 108.3 jit_solution(7463207992026796405)
XLA Ops:
  0.0 103.5 %shard_map.37 = f32[1024,1024]{1,0:T(8,128)} custom-call(f32[128,1024]{1,0:T(8,128)} %map_ref.1, f32[1,128]{1,0:T(1,128)} %bitcast.2, s32[1,128]{1,0:T(1,128)} %bitcast.3), custom_call_target="tpu_custom_call" | custom-call | flops 4294967296 | bytes 8388608 | tf_op jit(solution)/shard_map/pallas_call | solution.py:382
  103.5 4.8 %copy.5 = f32[1024,1024]{1,0:T(8,128)} copy(f32[1024,1024]{1,0:T(8,128)} %shard_map.37) | data formatting | bytes 8388608

commit v2 on v1

v2 whole, which is shorter than its diff:
```python
import functools

import jax
import jax.numpy as jnp
from jax import lax
from jax.experimental import pallas as pl
from jax.experimental.pallas import tpu as pltpu
from jax.sharding import PartitionSpec as P

MESH = pl.DeviceIdType.MESH
OBS, SIDE = 2048, 1024
PIECE, STEPS, CUTS = 16, 5, 8
SLOTS = STEPS * CUTS
TRIO = 3 * PIECE
LEFT = OBS

PARENT = ((0, 0, 0), (1, 3, 1), (4, 2, 4), (7, 8, 8), (9, 12, 10))

OUTER = (
    tuple((i, i) for i in range(0, 4)),
    tuple((i, i) for i in range(4, 7)),
    tuple((i, i) for i in range(7, 10)),
    tuple((i, i) for i in range(10, 13)),
    tuple((i, i) for i in range(13, 16)),
)
INNER = (
    ((0, 3), (3, 0), (6, 1), (5, 2)),
    ((1, 6), (2, 5), (9, 4)),
    ((4, 9), (12, 8), (13, 7)),
    ((8, 12), (14, 11), (15, 10)),
    ((7, 13), (11, 14), (10, 15)),
)
HOP = 3
LAG = 4 * HOP + 1
STARTS = (LAG, CUTS + LAG, max(4 * CUTS, 2 * CUTS + LAG), 3 * CUTS + LAG, 4 * CUTS + LAG)
FIRST_ROWS = (0, 512, 896, 1280, 1664)
TURNS = STARTS[-1] + CUTS
DOTS = (
    STARTS[0] + 3, STARTS[0] + 7, STARTS[1] + 5, STARTS[2] + 2, STARTS[2] + 7,
    max(STARTS[3] + 5, STARTS[2] + 11), max(STARTS[4] + 2, STARTS[3] + 9), STARTS[4] + 7,
)


def base_of(block):
    return 128 + CUTS * TRIO * ((block - 1) // 3) + PIECE * ((block - 1) % 3)


def row_of(block, cut):
    return PIECE * cut if block == 0 else base_of(block) + TRIO * cut


def pick(choice, values):
    out = values[-1]
    for i in reversed(range(len(values) - 1)):
        out = jnp.where(choice == i, values[i], out)
    return out


def kernel(
    map_ref, weights_ref, mask_ref, total,
    store, relay, weights, mask, scales, columns, right_hi, right_lo, left_hi, left_lo,
    small_sem, load_sem, slot_sem, left_sem, relay_sem, scale_sem,
    sent_sem, sent_scale_sem, plus_sem, minus_sem, twin_sem, cross_sem, toward_sem, onward_sem,
):
    row, col = lax.axis_index("row"), lax.axis_index("col")
    x_lo, z = row // 8, row % 8
    x_hi, y, core = col // 8, (col // 2) % 4, col % 2
    up = (x_lo * 8 + (z + 1) % 8, col)
    down = (x_lo * 8 + (z + 7) % 8, col)
    pair = ((1 - x_lo) * 8 + z, col)
    twin = (row, x_hi * 8 + y * 2 + (1 - core))
    plus_0, plus = ((row, x_hi * 8 + ((y + 1) % 4) * 2 + n) for n in range(2))
    minus_0, minus = ((row, x_hi * 8 + ((y + 3) % 4) * 2 + n) for n in range(2))
    across_0, across = (((1 - x_lo) * 8 + z, (1 - x_hi) * 8 + y * 2 + n) for n in range(2))
    links = (up, down, pair)
    outer = x_hi == x_lo
    inner = x_hi != x_lo
    dy = (y + 4 - z // 2) % 4
    owner = (dy == 0) & (core == z % 2)
    first = jnp.where(outer & (dy == 0), core == z % 2, core == 1)

    def loading(cut):
        rows = pl.ds(PIECE * cut, PIECE)
        return pltpu.make_async_copy(map_ref.at[rows], store.at[rows], load_sem.at[cut])

    for cut in range(CUTS):
        loading(cut).start()
    small = (
        pltpu.make_async_copy(weights_ref, weights, small_sem.at[0]),
        pltpu.make_async_copy(mask_ref, mask, small_sem.at[1]),
    )
    for one in small:
        one.start()

    barrier = pltpu.get_barrier_semaphore()
    for other in (up, down, pair, twin, plus_0, plus, minus_0, minus, across_0, across):
        pl.semaphore_signal(barrier, inc=1, device_id=other, device_id_type=MESH)
    for one in small:
        one.wait()
    scales[pl.ds(0, 8), :] = jnp.broadcast_to(weights[...] * mask[...].astype(jnp.float32), (8, 128))
    pl.semaphore_wait(barrier, 10)

    def remote(source, target, sent, arrived, device):
        return pltpu.make_async_remote_copy(
            src_ref=source, dst_ref=target, send_sem=sent, recv_sem=arrived,
            device_id=device, device_id_type=MESH,
        )

    def arrival(ref, sem):
        return remote(ref, ref, sent_sem.at[0], sem, up)

    def span(start, size):
        return store.at[pl.ds(pl.multiple_of(start, 8), size)]

    def send_scale(source_block, step, g):
        remote(
            scales.at[pl.ds(8 * source_block, 8)],
            scales.at[pl.ds(pl.multiple_of(8 * (3 * step + 1 + g), 8), 8)],
            sent_scale_sem.at[0], scale_sem.at[step], links[g],
        ).start()

    for cut in range(CUTS):
        loading(cut).wait()
        if cut == 1:
            for g in range(3):
                send_scale(0, 0, g)
        for g in range(3):
            remote(
                span(PIECE * cut, PIECE), span(128 + TRIO * cut + PIECE * g, PIECE),
                sent_sem.at[0], slot_sem.at[cut], links[g],
            ).start()

    total[...] = jnp.zeros_like(total)

    def expand(block, start):
        square = jnp.broadcast_to(scales[pl.ds(pl.multiple_of(start, 8), 1), :], (128, 128))
        columns[block] = square.T

    back = (4 - dy) % 4
    hops = []
    for lane in range(4):
        on_outer = dy if lane % 2 == 0 else back
        on_inner = (1 + dy, 1 + back, pick(dy, (3, 2, 3, 4)), pick(dy, (3, 4, 3, 2)))[lane]
        hops.append(jnp.where(outer, on_outer, on_inner))
    goes_plus = (
        jnp.where(outer, dy <= 2, dy <= 2),
        inner & (dy < 0),
        jnp.where(outer, dy <= 2, (dy == 1) | (dy == 2)),
        inner & (dy == 3),
    )
    goes_minus = (
        inner & (dy < 0),
        jnp.where(outer, dy != 1, dy != 1),
        inner & (dy == 1),
        jnp.where(outer, dy != 1, (dy == 2) | (dy == 3)),
    )
    at_source = outer & owner
    from_row = jnp.where(at_source, 0, LEFT)

    def piece_of(slot, lane):
        third = (slot + 40 + lane) % 4
        there = (slot >= 0) & (slot < SLOTS) & ((third < 3) | (slot < CUTS))
        return jnp.where(third == 3, PIECE * slot, 128 + TRIO * slot + PIECE * third), there

    def pass_on(slot, lane, source_row, device, sent):
        at, _ = piece_of(slot, lane)
        remote(span(source_row + at, PIECE), span(LEFT + at, PIECE), sent, left_sem.at[lane, slot], device).start()

    def held(slot):
        return relay.at[pl.ds(pl.multiple_of(PIECE * slot, 8), PIECE)]

    def into_relay(slot, lane, device, sent):
        at, _ = piece_of(slot, lane)
        remote(span(at, PIECE), held(slot), sent, relay_sem.at[slot], device).start()

    def out_of_relay(slot, lane):
        at, _ = piece_of(slot, lane)
        arrival(held(slot), relay_sem.at[slot]).wait_recv()
        remote(held(slot), span(LEFT + at, PIECE), onward_sem.at[0], left_sem.at[lane, slot], across).start()

    def split(turn, start, phase, base, pieces):
        cut = turn - start

        @pl.when((turn >= start) & (turn < start + CUTS))
        def _():
            for n in range(pieces):
                (right_o, left_o), (right_i, left_i) = OUTER[phase][n], INNER[phase][n]

                def start_of(a, b):
                    def one(block):
                        return PIECE * cut if block == 0 else base_of(block) + TRIO * cut

                    return one(a) if a == b else jnp.where(outer, one(a), one(b))

                right_row = pl.multiple_of(start_of(right_o, right_i), 8)
                left_row = pl.multiple_of(LEFT + start_of(left_o, left_i), 8)
                block = right_o if right_o == right_i else jnp.where(outer, right_o, right_i)
                put = pl.ds(pl.multiple_of(base + PIECE * (pieces * cut + n), 16), PIECE)
                factor = columns[block, pl.ds(pl.multiple_of(PIECE * cut, 8), PIECE), :]
                for lane in range(SIDE // 128):
                    at = pl.ds(128 * lane, 128)
                    value = store[pl.ds(right_row, PIECE), at] * factor
                    high = value.astype(jnp.bfloat16)
                    right_hi[put, at] = high
                    right_lo[put, at] = (value - high.astype(jnp.float32)).astype(jnp.bfloat16)
                left_from = jnp.where(at_source, left_row - LEFT, left_row)
                value = store[pl.ds(pl.multiple_of(left_from, 8), PIECE), :]
                high = value.astype(jnp.bfloat16)
                left_hi[put, :] = high
                left_lo[put, :] = (value - high.astype(jnp.float32)).astype(jnp.bfloat16)

    def multiply(unit, n):
        k = pl.ds(pl.multiple_of(256 * unit, 256), 256)
        at = pl.ds(pl.multiple_of(256 * n, 256), 256)

        def product(a, b):
            return lax.dot_general(
                a[k, :], b[k, at], (((0,), (0,)), ((), ())), preferred_element_type=jnp.float32
            )

        total[:, at] += product(left_hi, right_hi) + product(left_hi, right_lo) + product(left_lo, right_hi)

    @pl.loop(0, TURNS)
    def _(turn):
        step, cut = turn // CUTS, turn % CUTS

        @pl.when(turn < SLOTS)
        def _():
            arrival(span(128 + TRIO * turn, TRIO), slot_sem.at[turn]).wait_recv()

            @pl.when(cut == 0)
            def _():
                arrival(scales.at[pl.ds(pl.multiple_of(8 + 24 * step, 8), 24)], scale_sem.at[step]).wait_recv()
                for g in range(3):
                    @pl.when(step < STEPS - 1)
                    def _():
                        source = pick(step, tuple(PARENT[s][g] for s in range(1, STEPS)))
                        remote(
                            scales.at[pl.ds(pl.multiple_of(8 * source, 8), 8)],
                            scales.at[pl.ds(pl.multiple_of(8 * (3 * step + 4 + g), 8), 8)],
                            sent_scale_sem.at[0], scale_sem.at[step + 1], links[g],
                        ).start()

            @pl.when(step < STEPS - 1)
            def _():
                for g in range(3):
                    base = pick(step, tuple(base_of(PARENT[s][g]) for s in range(1, STEPS)))
                    remote(
                        span(base + TRIO * cut, PIECE), span(128 + TRIO * (turn + CUTS) + PIECE * g, PIECE),
                        sent_sem.at[step + 1], slot_sem.at[turn + CUTS], links[g],
                    ).start()

            @pl.when(inner & owner)
            def _():
                for lane in range(4):
                    @pl.when(piece_of(turn, lane)[1])
                    def _():
                        if lane < 2:
                            pass_on(turn, lane, 0, across, cross_sem.at[0])
                        else:
                            into_relay(turn, lane, (plus, minus)[lane - 2], toward_sem.at[lane - 2])

        for lane, place in ((2, 1), (3, 3)):
            slot = turn - HOP

            @pl.when(inner & first & (dy == place) & piece_of(slot, lane)[1])
            def _():
                out_of_relay(slot, lane)

        for lane in range(4):
            slot = turn - HOP * hops[lane] - jnp.where(first, 0, 1)
            at, there = piece_of(slot, lane)

            @pl.when(there)
            def _():
                @pl.when(jnp.logical_not(at_source))
                def _():
                    arrival(span(LEFT + at, PIECE), left_sem.at[lane, slot]).wait_recv()

                @pl.when(first & goes_plus[lane])
                def _():
                    pass_on(slot, lane, from_row, plus, plus_sem.at[lane])

                @pl.when(first & goes_minus[lane])
                def _():
                    pass_on(slot, lane, from_row, minus, minus_sem.at[lane])

                @pl.when(first)
                def _():
                    pass_on(slot, lane, from_row, twin, twin_sem.at[lane])

        for phase, blocks in ((0, range(7)), (1, range(7, 10)), (2, range(10, 16))):
            @pl.when(turn == STARTS[phase])
            def _():
                for block in blocks:
                    expand(block, 8 * block)

        for phase in range(5):
            split(turn, STARTS[phase], phase, FIRST_ROWS[phase], len(OUTER[phase]))

        unit, begun = 0, DOTS[0]
        for number, at in enumerate(DOTS):
            unit = jnp.where(turn >= at, number, unit)
            begun = jnp.where(turn >= at, at, begun)
        quarter = turn - begun
        last = unit == len(DOTS) - 1

        @pl.when((quarter >= 0) & (quarter < 4))
        def _():
            @pl.loop(quarter, jnp.where(last, 4, quarter + 1))
            def _(n):
                multiply(unit, n)

    for step in range(STEPS):
        remote(
            span(0, CUTS * TRIO), span(0, CUTS * TRIO), sent_sem.at[step], slot_sem.at[0], up
        ).wait_send()
    remote(
        scales.at[pl.ds(8, 120)], scales.at[pl.ds(8, 120)], sent_scale_sem.at[0], slot_sem.at[0], up
    ).wait_send()

    def drain(sem, rows):
        remote(span(0, rows), span(0, rows), sem, slot_sem.at[0], up).wait_send()

    for lane in range(4):
        @pl.when(first & goes_plus[lane])
        def _():
            drain(plus_sem.at[lane], 512)

        @pl.when(first & goes_minus[lane])
        def _():
            drain(minus_sem.at[lane], 512)

        @pl.when(first)
        def _():
            drain(twin_sem.at[lane], 512)

    @pl.when(inner & owner)
    def _():
        drain(cross_sem.at[0], 1024)
        drain(toward_sem.at[0], 512)
        drain(toward_sem.at[1], 512)

    @pl.when(inner & first & ((dy == 1) | (dy == 3)))
    def _():
        drain(onward_sem.at[0], 512)


def per_device(forward_map, sensor_weights, sensor_mask):
    dma = pltpu.SemaphoreType.DMA
    half = pltpu.VMEM((OBS, SIDE), jnp.bfloat16)
    return pl.pallas_call(
        kernel,
        out_shape=pltpu.VMEM((SIDE, SIDE), jnp.float32),
        in_specs=[
            pl.BlockSpec(memory_space=pltpu.HBM),
            pl.BlockSpec(memory_space=pltpu.HBM),
            pl.BlockSpec(memory_space=pltpu.HBM),
        ],
        out_specs=pl.BlockSpec(memory_space=pltpu.VMEM),
        scratch_shapes=[
            pltpu.VMEM((2 * OBS, SIDE), jnp.float32),
            pltpu.VMEM((PIECE * SLOTS, SIDE), jnp.float32),
            pltpu.VMEM((1, 128), jnp.float32),
            pltpu.VMEM((1, 128), jnp.int32),
            pltpu.VMEM((128, 128), jnp.float32),
            pltpu.VMEM((16, 128, 128), jnp.float32),
            half, half, half, half,
            dma((2,)), dma((CUTS,)), dma((SLOTS,)), dma((4, SLOTS)), dma((SLOTS,)), dma((STEPS,)),
            dma((STEPS,)), dma((1,)), dma((4,)), dma((4,)), dma((4,)), dma((1,)), dma((2,)), dma((1,)),
        ],
        compiler_params=pltpu.CompilerParams(
            collective_id=0, has_side_effects=True, vmem_limit_bytes=67043328 - 4 * SIDE * SIDE
        ),
        cost_estimate=pl.CostEstimate(
            flops=2 * OBS * SIDE * SIDE, bytes_accessed=8 * SIDE * SIDE, transcendentals=0
        ),
    )(forward_map, sensor_weights.reshape(1, -1), sensor_mask.reshape(1, -1))


def solution(mesh):
    placed = (P("row", "col"), P("row"), P("row"))
    return jax.shard_map(
        per_device, mesh=mesh, in_specs=placed, out_specs=P("row", "col"), check_vma=False
    )
```

time: 108 us -> 87.9 us (0.81); the launches traced: 108 us -> 87 us
  Pallas kernels: 103 us -> 85 us
  local copies, waits for them, and re-layouts: 4.79 us -> 2.02 us
    pallas_call x1, Pallas kernels: 103 us -> 85 us  [per_device(): pl.pallas_call(kernel, out_shape=pltpu.VMEM((SIDE, SIDE), jnp.float32), i...]
    unnamed x1, local copies, waits for them, and re-layouts: 4.79 us -> 2.02 us
where the time goes in v2:
time: 87.9 us; the launch traced here: 87 us
  Pallas kernels  85 us (97%)
  local copies, waits for them, and re-layouts  2.02 us (2%)
    pallas_call x1, Pallas kernels, per_device(): pl.pallas_call(kernel, out_shape=pltpu.VMEM((SIDE, SIDE), jnp.float32), i...  85 us
    unnamed x1, local copies, waits for them, and re-layouts  2.02 us

profile of v2, /device:TPU:10, one launch (start us, length us, event | category | flops | bytes accessed | tf_op | source)
XLA Modules:
  0.0 87.0 jit_solution(1938693058641661402)
XLA Ops:
  0.0 85.0 %shard_map.37 = f32[1024,1024]{1,0:T(8,128)S(1)} custom-call(f32[128,1024]{1,0:T(8,128)} %map_ref.1, f32[1,128]{1,0:T(1,128)} %bitcast.2, s32[1,128]{1,0:T(1,128)} %bitcast.3), custom_call_target="tpu_custom_call" | custom-call | flops 4294967296 | bytes 8388608 | tf_op jit(solution)/shard_map/pallas_call | solution.py:352
  85.0 2.0 %copy.5 = f32[1024,1024]{1,0:T(8,128)} copy(f32[1024,1024]{1,0:T(8,128)S(1)} %shard_map.37) | data formatting | bytes 8388608

commit v3 on v2

--- a/solution.py
+++ b/solution.py
@@ -16,29 +16,45 @@
 
 PARENT = ((0, 0, 0), (1, 3, 1), (4, 2, 4), (7, 8, 8), (9, 12, 10))
 
-OUTER = (
-    tuple((i, i) for i in range(0, 4)),
-    tuple((i, i) for i in range(4, 7)),
-    tuple((i, i) for i in range(7, 10)),
-    tuple((i, i) for i in range(10, 13)),
-    tuple((i, i) for i in range(13, 16)),
-)
+OUTER = tuple(tuple((i, i) for i in blocks) for blocks in (range(4), range(4, 7), range(7, 9), range(9, 13), range(13, 16)))
 INNER = (
     ((0, 3), (3, 0), (6, 1), (5, 2)),
     ((1, 6), (2, 5), (9, 4)),
-    ((4, 9), (12, 8), (13, 7)),
-    ((8, 12), (14, 11), (15, 10)),
+    ((4, 9), (12, 8)),
+    ((8, 12), (13, 7), (14, 11), (15, 10)),
     ((7, 13), (11, 14), (10, 15)),
 )
-HOP = 3
-LAG = 4 * HOP + 1
-STARTS = (LAG, CUTS + LAG, max(4 * CUTS, 2 * CUTS + LAG), 3 * CUTS + LAG, 4 * CUTS + LAG)
-FIRST_ROWS = (0, 512, 896, 1280, 1664)
-TURNS = STARTS[-1] + CUTS
-DOTS = (
-    STARTS[0] + 3, STARTS[0] + 7, STARTS[1] + 5, STARTS[2] + 2, STARTS[2] + 7,
-    max(STARTS[3] + 5, STARTS[2] + 11), max(STARTS[4] + 2, STARTS[3] + 9), STARTS[4] + 7,
-)
+WIDE = 256
+LATE = 38
+BEHIND = (0, 3, 5, 8, 10)
+LAG = BEHIND[4] + 1
+STARTS = (LAG, CUTS + LAG, 2 * CUTS + LAG, 3 * CUTS + LAG, 4 * CUTS + LAG)
+FIRST_ROWS = (0, 512, 896, 1152, 1664)
+SOONER = LAG - (BEHIND[3] + 1)
+TURNS = STARTS[-1] + CUTS - SOONER
+
+
+def rows_of(lane, first, end):
+    return PIECE * sum(slot < CUTS or (slot + lane) % 4 < 3 for slot in range(first, end))
+
+
+def dots():
+    begun, out = 0, []
+    for unit in range(7):
+        rows = 256 * (unit + 1)
+        group = max(n for n in range(5) if FIRST_ROWS[n] < rows)
+        full = -(-(rows - FIRST_ROWS[group]) // (PIECE * len(OUTER[group])))
+        begun = max(begun, STARTS[group] + full - 1)
+        for quarter in range(4):
+            out.append([begun + quarter, unit, quarter, 1])
+        begun += 4
+    out = [one for one in out if one[2] == 0 or one[0] >= TURNS - 1]
+    out = [one for one in out if one[0] < TURNS - 1] + TAIL
+    return tuple(map(tuple, out))
+
+
+TAIL = [[TURNS - 2, 6, 2, 2]]
+DOTS = dots()
 
 
 def base_of(block):
@@ -56,9 +72,33 @@
     return out
 
 
+def products(unit, at, right_hi, right_lo, left_hi, left_lo):
+    k = pl.ds(256 * unit if isinstance(unit, int) else pl.multiple_of(256 * unit, 256), 256)
+
+    def product(a, b):
+        return lax.dot_general(a[k, :], b[k, at], (((0,), (0,)), ((), ())), preferred_element_type=jnp.float32)
+
+    return product(left_hi, right_hi) + product(left_hi, right_lo) + product(left_lo, right_hi)
+
+
+def last_unit(total, right_hi, right_lo, left_hi, left_lo, gram_ref, done, out_sem):
+    def writing(n):
+        at = pl.ds(n * WIDE if isinstance(n, int) else pl.multiple_of(n * WIDE, WIDE), WIDE)
+        return pltpu.make_async_copy(done.at[n], gram_ref.at[:, at], out_sem.at[n])
+
+    @pl.loop(0, SIDE // WIDE)
+    def _(n):
+        at = pl.ds(pl.multiple_of(n * WIDE, WIDE), WIDE)
+        done[n] = total[:, at] + products(7, at, right_hi, right_lo, left_hi, left_lo)
+        writing(n).start()
+
+    for n in range(SIDE // WIDE):
+        writing(n).wait()
+
+
 def kernel(
-    map_ref, weights_ref, mask_ref, total,
-    store, relay, weights, mask, scales, columns, right_hi, right_lo, left_hi, left_lo,
+    map_ref, weights_ref, mask_ref, total, right_hi, right_lo, left_hi, left_lo,
+    store, relay, weights, mask, scales, columns,
     small_sem, load_sem, slot_sem, left_sem, relay_sem, scale_sem,
     sent_sem, sent_scale_sem, plus_sem, minus_sem, twin_sem, cross_sem, toward_sem, onward_sem,
 ):
@@ -142,6 +182,7 @@
         on_outer = dy if lane % 2 == 0 else back
         on_inner = (1 + dy, 1 + back, pick(dy, (3, 2, 3, 4)), pick(dy, (3, 4, 3, 2)))[lane]
         hops.append(jnp.where(outer, on_outer, on_inner))
+    late = [pick(hop, BEHIND) + jnp.where(first, 0, 1) for hop in hops]
     goes_plus = (
         jnp.where(outer, dy <= 2, dy <= 2),
         inner & (dy < 0),
@@ -155,33 +196,40 @@
         jnp.where(outer, dy != 1, (dy == 2) | (dy == 3)),
     )
     at_source = outer & owner
+    late_hops = jnp.where(outer, pick(dy, (0, 1, 2, 1)), pick(dy, (1, 2, 3, 2)))
+    late_by = pick(late_hops, BEHIND) + jnp.where(first, 0, 1)
+    ends = first & (dy == 0)
+    late_plus = (first & (dy <= 1), ends)
+    late_minus = (ends, first & ((dy == 0) | (dy == 3)))
     from_row = jnp.where(at_source, 0, LEFT)
+    waits = jnp.logical_not(at_source)
+    relays = inner & first & ((dy == 1) | (dy == 3))
+    crosses = inner & owner
+    sends_plus = [first & one for one in goes_plus]
+    sends_minus = [first & one for one in goes_minus]
 
     def piece_of(slot, lane):
-        third = (slot + 40 + lane) % 4
+        third = (slot + 40 + lane) & 3
         there = (slot >= 0) & (slot < SLOTS) & ((third < 3) | (slot < CUTS))
         return jnp.where(third == 3, PIECE * slot, 128 + TRIO * slot + PIECE * third), there
 
-    def pass_on(slot, lane, source_row, device, sent):
-        at, _ = piece_of(slot, lane)
+    def pass_on(slot, lane, at, source_row, device, sent):
         remote(span(source_row + at, PIECE), span(LEFT + at, PIECE), sent, left_sem.at[lane, slot], device).start()
 
     def held(slot):
         return relay.at[pl.ds(pl.multiple_of(PIECE * slot, 8), PIECE)]
 
-    def into_relay(slot, lane, device, sent):
-        at, _ = piece_of(slot, lane)
+    def into_relay(slot, at, device, sent):
         remote(span(at, PIECE), held(slot), sent, relay_sem.at[slot], device).start()
 
-    def out_of_relay(slot, lane):
-        at, _ = piece_of(slot, lane)
+    def out_of_relay(slot, lane, at):
         arrival(held(slot), relay_sem.at[slot]).wait_recv()
         remote(held(slot), span(LEFT + at, PIECE), onward_sem.at[0], left_sem.at[lane, slot], across).start()
 
-    def split(turn, start, phase, base, pieces):
+    def split(turn, start, phase, base, pieces, first_cut=0, end_cut=CUTS):
         cut = turn - start
 
-        @pl.when((turn >= start) & (turn < start + CUTS))
+        @pl.when((turn >= start + first_cut) & (turn < start + end_cut))
         def _():
             for n in range(pieces):
                 (right_o, left_o), (right_i, left_i) = OUTER[phase][n], INNER[phase][n]
@@ -210,19 +258,12 @@
                 left_lo[put, :] = (value - high.astype(jnp.float32)).astype(jnp.bfloat16)
 
     def multiply(unit, n):
-        k = pl.ds(pl.multiple_of(256 * unit, 256), 256)
         at = pl.ds(pl.multiple_of(256 * n, 256), 256)
-
-        def product(a, b):
-            return lax.dot_general(
-                a[k, :], b[k, at], (((0,), (0,)), ((), ())), preferred_element_type=jnp.float32
-            )
-
-        total[:, at] += product(left_hi, right_hi) + product(left_hi, right_lo) + product(left_lo, right_hi)
+        total[:, at] += products(unit, at, right_hi, right_lo, left_hi, left_lo)
 
     @pl.loop(0, TURNS)
     def _(turn):
-        step, cut = turn // CUTS, turn % CUTS
+        step, cut = turn >> 3, turn & 7
 
         @pl.when(turn < SLOTS)
         def _():
@@ -250,64 +291,89 @@
                         sent_sem.at[step + 1], slot_sem.at[turn + CUTS], links[g],
                     ).start()
 
-            @pl.when(inner & owner)
+            @pl.when(crosses)
             def _():
                 for lane in range(4):
-                    @pl.when(piece_of(turn, lane)[1])
+                    at, there = piece_of(turn, lane)
+
+                    @pl.when(there)
                     def _():
-                        if lane < 2:
-                            pass_on(turn, lane, 0, across, cross_sem.at[0])
-                        else:
-                            into_relay(turn, lane, (plus, minus)[lane - 2], toward_sem.at[lane - 2])
-
-        for lane, place in ((2, 1), (3, 3)):
-            slot = turn - HOP
-
-            @pl.when(inner & first & (dy == place) & piece_of(slot, lane)[1])
-            def _():
-                out_of_relay(slot, lane)
+                        @pl.when(turn >= LATE)
+                        def _():
+                            pass_on(turn, lane, at, 0, across, cross_sem.at[1])
+
+                        @pl.when(turn < LATE)
+                        def _():
+                            if lane < 2:
+                                pass_on(turn, lane, at, 0, across, cross_sem.at[0])
+                            else:
+                                into_relay(turn, at, (plus, minus)[lane - 2], toward_sem.at[lane - 2])
+
+        @pl.when(relays)
+        def _():
+            slot = turn - BEHIND[1]
+            for lane, place in ((2, 1), (3, 3)):
+                at, there = piece_of(slot, lane)
+
+                @pl.when((dy == place) & there & (slot < LATE))
+                def _():
+                    out_of_relay(slot, lane, at)
+
+        def forward(slot, lane, at, on_plus, on_minus, sems):
+            @pl.when(waits)
+            def _():
+                arrival(span(LEFT + at, PIECE), left_sem.at[lane, slot]).wait_recv()
+
+            @pl.when(on_plus)
+            def _():
+                pass_on(slot, lane, at, from_row, plus, plus_sem.at[sems + lane])
+
+            @pl.when(on_minus)
+            def _():
+                pass_on(slot, lane, at, from_row, minus, minus_sem.at[sems + lane])
+
+            @pl.when(first)
+            def _():
+                pass_on(slot, lane, at, from_row, twin, twin_sem.at[lane])
+
+        @pl.when((turn - late_by >= LATE) & (turn - late_by < SLOTS))
+        def _():
+            slot = turn - late_by
+            for lane in range(4):
+                at, there = piece_of(slot, lane)
+
+                @pl.when(there)
+                def _():
+                    forward(slot, lane, at, late_plus[lane % 2], late_minus[lane % 2], 4)
 
         for lane in range(4):
-            slot = turn - HOP * hops[lane] - jnp.where(first, 0, 1)
+            slot = turn - late[lane]
             at, there = piece_of(slot, lane)
 
-            @pl.when(there)
-            def _():
-                @pl.when(jnp.logical_not(at_source))
-                def _():
-                    arrival(span(LEFT + at, PIECE), left_sem.at[lane, slot]).wait_recv()
-
-                @pl.when(first & goes_plus[lane])
-                def _():
-                    pass_on(slot, lane, from_row, plus, plus_sem.at[lane])
-
-                @pl.when(first & goes_minus[lane])
-                def _():
-                    pass_on(slot, lane, from_row, minus, minus_sem.at[lane])
-
-                @pl.when(first)
-                def _():
-                    pass_on(slot, lane, from_row, twin, twin_sem.at[lane])
-
-        for phase, blocks in ((0, range(7)), (1, range(7, 10)), (2, range(10, 16))):
+            @pl.when(there & (slot < LATE))
+            def _():
+                forward(slot, lane, at, sends_plus[lane], sends_minus[lane], 0)
+
+        for phase, blocks in ((0, range(7)), (1, range(7, 10)), (2, range(10, 13)), (3, range(13, 16))):
             @pl.when(turn == STARTS[phase])
             def _():
                 for block in blocks:
                     expand(block, 8 * block)
 
-        for phase in range(5):
+        late_cut = LATE % CUTS
+        for phase in range(4):
             split(turn, STARTS[phase], phase, FIRST_ROWS[phase], len(OUTER[phase]))
-
-        unit, begun = 0, DOTS[0]
-        for number, at in enumerate(DOTS):
-            unit = jnp.where(turn >= at, number, unit)
-            begun = jnp.where(turn >= at, at, begun)
-        quarter = turn - begun
-        last = unit == len(DOTS) - 1
+        split(turn, STARTS[4], 4, FIRST_ROWS[4], len(OUTER[4]), 0, late_cut)
+        split(turn, STARTS[4] - SOONER, 4, FIRST_ROWS[4], len(OUTER[4]), late_cut, CUTS)
+
+        begun, unit, ahead, pace = DOTS[0]
+        for one in DOTS[1:]:
+            begun, unit, ahead, pace = (jnp.where(turn >= one[0], new, old) for new, old in zip(one, (begun, unit, ahead, pace)))
+        quarter = ahead + pace * (turn - begun)
 
         @pl.when((quarter >= 0) & (quarter < 4))
         def _():
-            @pl.loop(quarter, jnp.where(last, 4, quarter + 1))
+            @pl.loop(quarter, quarter + pace)
             def _(n):
                 multiply(unit, n)
 
@@ -323,41 +389,43 @@
         remote(span(0, rows), span(0, rows), sem, slot_sem.at[0], up).wait_send()
 
     for lane in range(4):
-        @pl.when(first & goes_plus[lane])
-        def _():
-            drain(plus_sem.at[lane], 512)
-
-        @pl.when(first & goes_minus[lane])
-        def _():
-            drain(minus_sem.at[lane], 512)
-
-        @pl.when(first)
-        def _():
-            drain(twin_sem.at[lane], 512)
-
-    @pl.when(inner & owner)
+        soon, later = rows_of(lane, 0, LATE), rows_of(lane, LATE, SLOTS)
+        for condition, sem, rows in (
+            (sends_plus[lane], plus_sem.at[lane], soon),
+            (sends_minus[lane], minus_sem.at[lane], soon),
+            (late_plus[lane % 2], plus_sem.at[4 + lane], later),
+            (late_minus[lane % 2], minus_sem.at[4 + lane], later),
+            (first, twin_sem.at[lane], soon + later),
+        ):
+            @pl.when(condition)
+            def _():
+                drain(sem, rows)
+
+    @pl.when(crosses)
     def _():
-        drain(cross_sem.at[0], 1024)
-        drain(toward_sem.at[0], 512)
-        drain(toward_sem.at[1], 512)
-
-    @pl.when(inner & first & ((dy == 1) | (dy == 3)))
-    def _():
-        drain(onward_sem.at[0], 512)
+        drain(cross_sem.at[0], rows_of(0, 0, LATE) + rows_of(1, 0, LATE))
+        drain(cross_sem.at[1], sum(rows_of(lane, LATE, SLOTS) for lane in range(4)))
+        drain(toward_sem.at[0], rows_of(2, 0, LATE))
+        drain(toward_sem.at[1], rows_of(3, 0, LATE))
+
+    for lane, place in ((2, 1), (3, 3)):
+        @pl.when(relays & (dy == place))
+        def _():
+            drain(onward_sem.at[0], rows_of(lane, 0, LATE))
 
 
 def per_device(forward_map, sensor_weights, sensor_mask):
     dma = pltpu.SemaphoreType.DMA
     half = pltpu.VMEM((OBS, SIDE), jnp.bfloat16)
-    return pl.pallas_call(
+    parts = pl.pallas_call(
         kernel,
-        out_shape=pltpu.VMEM((SIDE, SIDE), jnp.float32),
+        out_shape=(pltpu.VMEM((SIDE, SIDE), jnp.float32), half, half, half, half),
         in_specs=[
             pl.BlockSpec(memory_space=pltpu.HBM),
             pl.BlockSpec(memory_space=pltpu.HBM),
             pl.BlockSpec(memory_space=pltpu.HBM),
         ],
-        out_specs=pl.BlockSpec(memory_space=pltpu.VMEM),
+        out_specs=(pl.BlockSpec(memory_space=pltpu.VMEM),) * 5,
         scratch_shapes=[
             pltpu.VMEM((2 * OBS, SIDE), jnp.float32),
             pltpu.VMEM((PIECE * SLOTS, SIDE), jnp.float32),
@@ -365,17 +433,25 @@
             pltpu.VMEM((1, 128), jnp.int32),
             pltpu.VMEM((128, 128), jnp.float32),
             pltpu.VMEM((16, 128, 128), jnp.float32),
-            half, half, half, half,
             dma((2,)), dma((CUTS,)), dma((SLOTS,)), dma((4, SLOTS)), dma((SLOTS,)), dma((STEPS,)),
-            dma((STEPS,)), dma((1,)), dma((4,)), dma((4,)), dma((4,)), dma((1,)), dma((2,)), dma((1,)),
+            dma((STEPS,)), dma((1,)), dma((8,)), dma((8,)), dma((4,)), dma((2,)), dma((2,)), dma((1,)),
         ],
         compiler_params=pltpu.CompilerParams(
-            collective_id=0, has_side_effects=True, vmem_limit_bytes=67043328 - 4 * SIDE * SIDE
+            collective_id=0, has_side_effects=True, vmem_limit_bytes=67043328 - 20 * SIDE * SIDE
         ),
         cost_estimate=pl.CostEstimate(
             flops=2 * OBS * SIDE * SIDE, bytes_accessed=8 * SIDE * SIDE, transcendentals=0
         ),
     )(forward_map, sensor_weights.reshape(1, -1), sensor_mask.reshape(1, -1))
+    return pl.pallas_call(
+        last_unit,
+        out_shape=jax.ShapeDtypeStruct((SIDE, SIDE), jnp.float32),
+        in_specs=[pl.BlockSpec(memory_space=pltpu.VMEM)] * 5,
+        out_specs=pl.BlockSpec(memory_space=pl.ANY),
+        scratch_shapes=[pltpu.VMEM((SIDE // WIDE, SIDE, WIDE), jnp.float32), dma((SIDE // WIDE,))],
+        compiler_params=pltpu.CompilerParams(vmem_limit_bytes=16 * 1024 * 1024),
+        cost_estimate=pl.CostEstimate(flops=2 * 256 * SIDE * SIDE, bytes_accessed=4 * SIDE * SIDE, transcendentals=0),
+    )(*parts)
 
 
 def solution(mesh):

time: 87.9 us -> 85.6 us (0.974)
  local copies, waits for them, and re-layouts: 2.02 us -> 0 us
    unnamed x1 -> x0, local copies, waits for them, and re-layouts: 2.02 us -> none
    pallas_call x1 -> x2, Pallas kernels: 85 us -> 85.5 us  [the longest x1 82 us: per_device(): pl.pallas_call(kernel, out_shape=(pltpu.VMEM((SIDE, SIDE), jnp.float32),...]
where the time goes in v3:
time: 85.6 us; the launch traced here: 85.5 us
  Pallas kernels  85.5 us (100%)
    pallas_call x1, Pallas kernels, per_device(): pl.pallas_call(kernel, out_shape=(pltpu.VMEM((SIDE, SIDE), jnp.float32),...  82 us
    pallas_call x1, Pallas kernels, per_device(): pl.pallas_call(last_unit, out_shape=jax.ShapeDtypeStruct((SIDE, SIDE), jn...  3.54 us

profile of v3, /device:TPU:10, one launch (start us, length us, event | category | flops | bytes accessed | tf_op | source)
XLA Modules:
  0.0 85.5 jit_solution(5936843114063945959)
XLA Ops:
  0.0 82.0 %shard_map.37 = (f32[1024,1024]{1,0:T(8,128)S(1)}, bf16[2048,1024]{1,0:T(8,128)(2,1)S(1)}, bf16[2048,1024]{1,0:T(8,128)(2,1)S(1)}, bf16[2048,1024]{1,0:T(8,128)(2,1)S(1)}, bf16[2048,1024]{1,0:T(8,128)(2,1)S(1)}) custom-call(f32[128,1024]{1,0:T(8,128)} %map_ref.1, f32[1,128]{1,0:T(1,128)} %bitcast.2, s32[1,128]{1,0:T(1,128)} %bitcast.3), custom_call_target="tpu_custom_call" | custom-call | flops 4294967296 | bytes 8388608 | tf_op jit(solution)/shard_map/pallas_call | solution.py:420
  82.0 3.5 %shard_map.38 = f32[1024,1024]{1,0:T(8,128)} custom-call(f32[1024,1024]{1,0:T(8,128)S(1)} %get-tuple-element.10.total, bf16[2048,1024]{1,0:T(8,128)(2,1)S(1)} %get-tuple-element.11.right_hi, bf16[2048,1024]{1,0:T(8,128)(2,1)S(1)} %get-tuple-element.12.right_lo, bf16[2048,1024]{1,0:T(8,128)(2,1)S(1)} %get-tuple-element.13.left_hi, ...), custom_call_target="tpu_custom_call" | custom-call | flops 536870912 | bytes 4194304 | tf_op jit(solution)/shard_map/pallas_call | solution.py:446

commit v4 on v3

--- a/solution.py
+++ b/solution.py
@@ -24,7 +24,7 @@
     ((8, 12), (13, 7), (14, 11), (15, 10)),
     ((7, 13), (11, 14), (10, 15)),
 )
-WIDE = 256
+WIDE = 512
 LATE = 38
 BEHIND = (0, 3, 5, 8, 10)
 LAG = BEHIND[4] + 1
@@ -261,54 +261,51 @@
         at = pl.ds(pl.multiple_of(256 * n, 256), 256)
         total[:, at] += products(unit, at, right_hi, right_lo, left_hi, left_lo)
 
-    @pl.loop(0, TURNS)
-    def _(turn):
+    def gathering(turn):
         step, cut = turn >> 3, turn & 7
-
-        @pl.when(turn < SLOTS)
-        def _():
-            arrival(span(128 + TRIO * turn, TRIO), slot_sem.at[turn]).wait_recv()
-
-            @pl.when(cut == 0)
-            def _():
-                arrival(scales.at[pl.ds(pl.multiple_of(8 + 24 * step, 8), 24)], scale_sem.at[step]).wait_recv()
-                for g in range(3):
-                    @pl.when(step < STEPS - 1)
+        arrival(span(128 + TRIO * turn, TRIO), slot_sem.at[turn]).wait_recv()
+
+        @pl.when(cut == 0)
+        def _():
+            arrival(scales.at[pl.ds(pl.multiple_of(8 + 24 * step, 8), 24)], scale_sem.at[step]).wait_recv()
+            for g in range(3):
+                @pl.when(step < STEPS - 1)
+                def _():
+                    source = pick(step, tuple(PARENT[s][g] for s in range(1, STEPS)))
+                    remote(
+                        scales.at[pl.ds(pl.multiple_of(8 * source, 8), 8)],
+                        scales.at[pl.ds(pl.multiple_of(8 * (3 * step + 4 + g), 8), 8)],
+                        sent_scale_sem.at[0], scale_sem.at[step + 1], links[g],
+                    ).start()
+
+        @pl.when(step < STEPS - 1)
+        def _():
+            for g in range(3):
+                base = pick(step, tuple(base_of(PARENT[s][g]) for s in range(1, STEPS)))
+                remote(
+                    span(base + TRIO * cut, PIECE), span(128 + TRIO * (turn + CUTS) + PIECE * g, PIECE),
+                    sent_sem.at[step + 1], slot_sem.at[turn + CUTS], links[g],
+                ).start()
+
+        @pl.when(crosses)
+        def _():
+            for lane in range(4):
+                at, there = piece_of(turn, lane)
+
+                @pl.when(there)
+                def _():
+                    @pl.when(turn >= LATE)
                     def _():
-                        source = pick(step, tuple(PARENT[s][g] for s in range(1, STEPS)))
-                        remote(
-                            scales.at[pl.ds(pl.multiple_of(8 * source, 8), 8)],
-                            scales.at[pl.ds(pl.multiple_of(8 * (3 * step + 4 + g), 8), 8)],
-                            sent_scale_sem.at[0], scale_sem.at[step + 1], links[g],
-                        ).start()
-
-            @pl.when(step < STEPS - 1)
-            def _():
-                for g in range(3):
-                    base = pick(step, tuple(base_of(PARENT[s][g]) for s in range(1, STEPS)))
-                    remote(
-                        span(base + TRIO * cut, PIECE), span(128 + TRIO * (turn + CUTS) + PIECE * g, PIECE),
-                        sent_sem.at[step + 1], slot_sem.at[turn + CUTS], links[g],
-                    ).start()
-
-            @pl.when(crosses)
-            def _():
-                for lane in range(4):
-                    at, there = piece_of(turn, lane)
-
-                    @pl.when(there)
+                        pass_on(turn, lane, at, 0, across, cross_sem.at[1])
+
+                    @pl.when(turn < LATE)
                     def _():
-                        @pl.when(turn >= LATE)
-                        def _():
-                            pass_on(turn, lane, at, 0, across, cross_sem.at[1])
-
-                        @pl.when(turn < LATE)
-                        def _():
-                            if lane < 2:
-                                pass_on(turn, lane, at, 0, across, cross_sem.at[0])
-                            else:
-                                into_relay(turn, at, (plus, minus)[lane - 2], toward_sem.at[lane - 2])
-
+                        if lane < 2:
+                            pass_on(turn, lane, at, 0, across, cross_sem.at[0])
+                        else:
+                            into_relay(turn, at, (plus, minus)[lane - 2], toward_sem.at[lane - 2])
+
+    def rest_of(turn, first_turn, end_turn):
         @pl.when(relays)
         def _():
             slot = turn - BEHIND[1]
@@ -336,7 +333,9 @@
             def _():
                 pass_on(slot, lane, at, from_row, twin, twin_sem.at[lane])
 
-        @pl.when((turn - late_by >= LATE) & (turn - late_by < SLOTS))
+        is_late = (turn - late_by >= LATE) & (turn - late_by < SLOTS)
+
+        @pl.when(is_late)
         def _():
             slot = turn - late_by
             for lane in range(4):
@@ -355,19 +354,24 @@
                 forward(slot, lane, at, sends_plus[lane], sends_minus[lane], 0)
 
         for phase, blocks in ((0, range(7)), (1, range(7, 10)), (2, range(10, 13)), (3, range(13, 16))):
-            @pl.when(turn == STARTS[phase])
-            def _():
-                for block in blocks:
-                    expand(block, 8 * block)
+            if first_turn <= STARTS[phase] < end_turn:
+                @pl.when(turn == STARTS[phase])
+                def _():
+                    for block in blocks:
+                        expand(block, 8 * block)
 
         late_cut = LATE % CUTS
-        for phase in range(4):
-            split(turn, STARTS[phase], phase, FIRST_ROWS[phase], len(OUTER[phase]))
-        split(turn, STARTS[4], 4, FIRST_ROWS[4], len(OUTER[4]), 0, late_cut)
-        split(turn, STARTS[4] - SOONER, 4, FIRST_ROWS[4], len(OUTER[4]), late_cut, CUTS)
-
-        begun, unit, ahead, pace = DOTS[0]
-        for one in DOTS[1:]:
+        for phase, sooner, first_cut, end_cut in (
+            (0, 0, 0, CUTS), (1, 0, 0, CUTS), (2, 0, 0, CUTS), (3, 0, 0, CUTS),
+            (4, 0, 0, late_cut), (4, SOONER, late_cut, CUTS),
+        ):
+            start = STARTS[phase] - sooner
+            if start + first_cut < end_turn and start + end_cut > first_turn:
+                split(turn, start, phase, FIRST_ROWS[phase], len(OUTER[phase]), first_cut, end_cut)
+
+        dots_here = [one for n, one in enumerate(DOTS) if one[0] < end_turn and (n + 1 == len(DOTS) or DOTS[n + 1][0] > first_turn)]
+        begun, unit, ahead, pace = dots_here[0]
+        for one in dots_here[1:]:
             begun, unit, ahead, pace = (jnp.where(turn >= one[0], new, old) for new, old in zip(one, (begun, unit, ahead, pace)))
         quarter = ahead + pace * (turn - begun)
 
@@ -376,6 +380,15 @@
             @pl.loop(quarter, quarter + pace)
             def _(n):
                 multiply(unit, n)
+
+    @pl.loop(0, SLOTS)
+    def _(turn):
+        gathering(turn)
+        rest_of(turn, 0, SLOTS)
+
+    @pl.loop(SLOTS, TURNS)
+    def _(turn):
+        rest_of(turn, SLOTS, TURNS)
 
     for step in range(STEPS):
         remote(

time: 85.6 us -> 85.2 us (level)
  no operation moved by 1% of the time
where the time goes in v4:
time: 85.2 us; the launch traced here: 85.1 us
  Pallas kernels  85.1 us (100%)
    pallas_call x1, Pallas kernels, per_device(): pl.pallas_call(kernel, out_shape=(pltpu.VMEM((SIDE, SIDE), jnp.float32),...  81.7 us
    pallas_call x1, Pallas kernels, per_device(): pl.pallas_call(last_unit, out_shape=jax.ShapeDtypeStruct((SIDE, SIDE), jn...  3.37 us

profile of v4, /device:TPU:10, one launch (start us, length us, event | category | flops | bytes accessed | tf_op | source)
XLA Modules:
  0.0 85.1 jit_solution(189908892595216204)
XLA Ops:
  0.0 81.7 %shard_map.37 = (f32[1024,1024]{1,0:T(8,128)S(1)}, bf16[2048,1024]{1,0:T(8,128)(2,1)S(1)}, bf16[2048,1024]{1,0:T(8,128)(2,1)S(1)}, bf16[2048,1024]{1,0:T(8,128)(2,1)S(1)}, bf16[2048,1024]{1,0:T(8,128)(2,1)S(1)}) custom-call(f32[128,1024]{1,0:T(8,128)} %map_ref.1, f32[1,128]{1,0:T(1,128)} %bitcast.2, s32[1,128]{1,0:T(1,128)} %bitcast.3), custom_call_target="tpu_custom_call" | custom-call | flops 4294967296 | bytes 8388608 | tf_op jit(solution)/shard_map/pallas_call | solution.py:433
  81.7 3.4 %shard_map.38 = f32[1024,1024]{1,0:T(8,128)} custom-call(f32[1024,1024]{1,0:T(8,128)S(1)} %get-tuple-element.10.total, bf16[2048,1024]{1,0:T(8,128)(2,1)S(1)} %get-tuple-element.11.right_hi, bf16[2048,1024]{1,0:T(8,128)(2,1)S(1)} %get-tuple-element.12.right_lo, bf16[2048,1024]{1,0:T(8,128)(2,1)S(1)} %get-tuple-element.13.left_hi, ...), custom_call_target="tpu_custom_call" | custom-call | flops 536870912 | bytes 4194304 | tf_op jit(solution)/shard_map/pallas_call | solution.py:459

commit v5 on v4

--- a/solution.py
+++ b/solution.py
@@ -86,10 +86,15 @@
         at = pl.ds(n * WIDE if isinstance(n, int) else pl.multiple_of(n * WIDE, WIDE), WIDE)
         return pltpu.make_async_copy(done.at[n], gram_ref.at[:, at], out_sem.at[n])
 
-    @pl.loop(0, SIDE // WIDE)
-    def _(n):
-        at = pl.ds(pl.multiple_of(n * WIDE, WIDE), WIDE)
-        done[n] = total[:, at] + products(7, at, right_hi, right_lo, left_hi, left_lo)
+    k = pl.ds(256 * 7, 256)
+    high, low = left_hi[k, :].T, left_lo[k, :].T
+    for n in range(SIDE // WIDE):
+        at = pl.ds(n * WIDE, WIDE)
+
+        def product(a, b):
+            return jnp.dot(a, b[k, at], preferred_element_type=jnp.float32)
+
+        done[n] = total[:, at] + product(high, right_hi) + product(high, right_lo) + product(low, right_hi)
         writing(n).start()
 
     for n in range(SIDE // WIDE):

time: 85.2 us -> 85 us (level)
  no operation moved by 1% of the time
where the time goes in v5:
time: 85 us; the launch traced here: 84.9 us
  Pallas kernels  84.9 us (100%)
    pallas_call x1, Pallas kernels, per_device(): pl.pallas_call(kernel, out_shape=(pltpu.VMEM((SIDE, SIDE), jnp.float32),...  81.7 us
    pallas_call x1, Pallas kernels, per_device(): pl.pallas_call(last_unit, out_shape=jax.ShapeDtypeStruct((SIDE, SIDE), jn...  3.17 us

profile of v5, /device:TPU:10, one launch (start us, length us, event | category | flops | bytes accessed | tf_op | source)
XLA Modules:
  0.0 84.9 jit_solution(13309758905571343475)
XLA Ops:
  0.0 81.7 %shard_map.37 = (f32[1024,1024]{1,0:T(8,128)S(1)}, bf16[2048,1024]{1,0:T(8,128)(2,1)S(1)}, bf16[2048,1024]{1,0:T(8,128)(2,1)S(1)}, bf16[2048,1024]{1,0:T(8,128)(2,1)S(1)}, bf16[2048,1024]{1,0:T(8,128)(2,1)S(1)}) custom-call(f32[128,1024]{1,0:T(8,128)} %map_ref.1, f32[1,128]{1,0:T(1,128)} %bitcast.2, s32[1,128]{1,0:T(1,128)} %bitcast.3), custom_call_target="tpu_custom_call" | custom-call | flops 4294967296 | bytes 8388608 | tf_op jit(solution)/shard_map/pallas_call | solution.py:438
  81.7 3.2 %shard_map.38 = f32[1024,1024]{1,0:T(8,128)} custom-call(f32[1024,1024]{1,0:T(8,128)S(1)} %get-tuple-element.10.total, bf16[2048,1024]{1,0:T(8,128)(2,1)S(1)} %get-tuple-element.11.right_hi, bf16[2048,1024]{1,0:T(8,128)(2,1)S(1)} %get-tuple-element.12.right_lo, bf16[2048,1024]{1,0:T(8,128)(2,1)S(1)} %get-tuple-element.13.left_hi, ...), custom_call_target="tpu_custom_call" | custom-call | flops 536870912 | bytes 4194304 | tf_op jit(solution)/shard_map/pallas_call | solution.py:464
